TPU v7x, 128 devices: a whole 4x4x4 slice. The times are simulated.
128 devices in a mesh: dp: 1, tp: 64 (over z, y, x), ep: 2 (over core).
Axes of the slice: x: 4, y: 4, z: 4, core: 2. Of those that a mesh axis runs over, the one named last changes fastest.
Arguments:
- tokens: bfloat16 [4096, 2048], P(('dp', 'ep', 'tp'))
- expert_ids: int32 [4096, 6], P(('dp', 'ep', 'tp'))
- gates: float32 [4096, 6], P(('dp', 'ep', 'tp'))
- slots: int32 [4096, 6], P(('dp', 'ep', 'tp'))
- shared_w1: bfloat16 [2048, 2816], P(None, 'tp')
- shared_w3: bfloat16 [2048, 2816], P(None, 'tp')
- shared_w2: bfloat16 [2816, 2048], P('tp')
- expert_w1: bfloat16 [64, 2048, 1408], P('ep')
- expert_w3: bfloat16 [64, 2048, 1408], P('ep')
- expert_w2: bfloat16 [64, 1408, 2048], P('ep')
Outputs:
- output: bfloat16 [4096, 2048], P(('dp', 'ep', 'tp'))
All inputs are finite; a program needn't handle non-finite values.
Results may differ from a plain program's by a relative error of at most 0.00145.
Values are sent between devices in bfloat16 or wider.
A program may use at most 1.5 GiB of HBM per device.

v0:
```python
import jax
import jax.numpy as jnp
from jax import lax
from jax.sharding import PartitionSpec as P


def capacity_rows(tok_dev, top_k, n_exp):
    return 8 * max(1, (2 * tok_dev * top_k + 8 * n_exp - 1) // (8 * n_exp))


def swiglu_rows(token_rows, w_gate, w_up, w_down):
    gate_pre = jnp.dot(token_rows, w_gate, preferred_element_type=jnp.float32)
    up_pre = jnp.dot(token_rows, w_up, preferred_element_type=jnp.float32)
    hidden = (jax.nn.silu(gate_pre) * up_pre).astype(jnp.bfloat16)
    return jnp.dot(hidden, w_down, preferred_element_type=jnp.float32)


def solution(mesh):
    ep_size = mesh.shape["ep"]
    row_spec = P(("dp", "ep", "tp"), None)
    expert_spec = P("ep", None, None)

    def local_layer(tokens, expert_ids, gates, slots, shared_w1, shared_w3, shared_w2, expert_w1, expert_w3, expert_w2):
        tok_dev, d_model = tokens.shape
        top_k = expert_ids.shape[1]
        local_exp = expert_w1.shape[0]
        cap_rows = capacity_rows(tok_dev, top_k, local_exp * ep_size)
        n_rows = local_exp * ep_size * cap_rows

        group_rows = lax.all_gather(tokens, "tp", axis=0, tiled=True)
        part_sum = swiglu_rows(group_rows, shared_w1, shared_w3, shared_w2)
        shared_out = lax.psum_scatter(part_sum, "tp", scatter_dimension=0, tiled=True)

        owner = expert_ids // local_exp
        row_code = (expert_ids % local_exp) * (ep_size * cap_rows) + owner * cap_rows + slots
        row_code = jnp.where(slots >= 0, row_code, n_rows)
        copy_tok = jnp.broadcast_to(jnp.arange(tok_dev, dtype=jnp.int32)[:, None], (tok_dev, top_k))
        inverse = jnp.full((n_rows,), tok_dev, jnp.int32).at[row_code.reshape(-1)].set(copy_tok.reshape(-1), mode="drop")
        send_rows = jnp.take(tokens, inverse, axis=0, mode="fill", fill_value=0).reshape(local_exp, ep_size, cap_rows, d_model)
        recv_rows = lax.all_to_all(send_rows, "ep", 1, 1, tiled=True)
        gate_pre = jnp.einsum("lscd,ldf->lscf", recv_rows, expert_w1, preferred_element_type=jnp.float32)
        up_pre = jnp.einsum("lscd,ldf->lscf", recv_rows, expert_w3, preferred_element_type=jnp.float32)
        hidden = (jax.nn.silu(gate_pre) * up_pre).astype(jnp.bfloat16)
        expert_out = jnp.einsum("lscf,lfd->lscd", hidden, expert_w2, preferred_element_type=jnp.float32).astype(jnp.bfloat16)
        back_rows = lax.all_to_all(expert_out, "ep", 1, 1, tiled=True).reshape(n_rows, d_model)
        routed = jnp.take(back_rows, row_code, axis=0, mode="fill", fill_value=0)
        routed_sum = jnp.sum(gates[:, :, None] * routed.astype(jnp.float32), axis=1)
        return (tokens.astype(jnp.float32) + shared_out + routed_sum).astype(jnp.bfloat16)

    return jax.shard_map(local_layer, mesh=mesh, in_specs=(row_spec, row_spec, row_spec, row_spec, P(None, "tp"), P(None, "tp"), P("tp", None), expert_spec, expert_spec, expert_spec), out_specs=row_spec, check_vma=False)
```

profile of v0, /device:TPU:0, one launch (start us, length us, event | category | flops | bytes accessed | tf_op | source)
XLA Modules:
  0.0 510.7 jit_solution(11196619561782449604)
XLA Ops:
  6.5 0.0 copy-start
  6.5 0.0 copy-start.1
  6.5 0.0 all-gather.2.cloned.1.call-start
  6.5 0.7 all-gather.2.cloned.1.call-update
  7.3 1.3 compare_and_fusion
  8.5 0.1 copy.19
  8.6 0.1 reshape.55
  8.7 0.1 reshape.78
  8.8 1.2 scatter_custom_fusion
  10.1 0.1 broadcast_in_dim.45
  10.2 0.0 copy-done.5
  10.2 0.0 copy-done.1
  10.2 2.5 gather_fusion
  12.7 1.6 copy_select_fusion
  14.3 0.0 copy-start.4
  14.3 3.9 all-to-all-start
  18.2 0.0 copy-start.3
  18.2 0.2 reduce-scatter.2.cloned.1.call-start
  18.4 72.4 %all-gather.2.cloned.1.call-done = bf16[2048,2048]{1,0:T(8,128)(2,1)} async-done(((bf16[32,2048]{1,0:T(8,128)(2,1)}), bf16[2048,2048]{1,0:T(8,128)(2,1)}) %all-gather.2.cloned.1.call-update) | async-done | bytes 8388624 | tf_op jit(solution)/shard_map/all_gather | solution.py:30
  90.8 0.0 copy-done.4
  90.8 6.0 %fusion.38 = f32[2048,44]{0,1:T(8,128)S(1)} fusion(bf16[2048,2048]{1,0:T(8,128)(2,1)} %all-gather.2.cloned.1.call-done, bf16[2048,44]{0,1:T(8,128)(2,1)S(1)} %copy-done.4), kind=kOutput, calls=%fused_computation.51 | convolution fusion | flops 369098752 | bytes 8929280 | tf_op jit(solution)/shard_map/dot_general | solution.py:12
  96.8 0.0 copy-done
  96.8 0.0 copy-done.3
  96.8 14.2 %fusion.18 = f32[2048,2048]{1,0:T(8,128)} fusion(bf16[44,2048]{1,0:T(8,128)(2,1)S(1)} %copy-done, bf16[2048,2048]{1,0:T(8,128)(2,1)} %all-gather.2.cloned.1.call-done, bf16[2048,44]{0,1:T(8,128)(2,1)S(1)} %copy-done.3, f32[2048,44]{0,1:T(8,128)S(1)} %fusion.38), kind=kOutput, calls=%fused_computation.18 | convolution fusion | flops 738738176 | bytes 25886720 | tf_op jit(solution)/shard_map/dot_general | solution.py:15
  111.1 0.0 reduce-scatter.2.cloned.1.call-update
  111.1 0.0 all-to-all-done
  111.1 59.7 %fusion.4 = f32[32,2,8,1408]{3,2,1,0:T(8,128)} fusion(bf16[32,2048,1408]{2,1,0:T(8,128)(2,1)} %param.17, bf16[32,2,8,2048]{3,2,0,1:T(8,128)(2,1)S(1)} %all-to-all-done), kind=kOutput, calls=%fused_computation.7 | convolution fusion | flops 2952790016 | bytes 189530112 | tf_op jit(solution)/shard_map/lscd,ldf->lscf/dot_general | solution.py:41
  170.8 60.7 %fusion.9 = bf16[32,2,8,1408]{3,2,1,0:T(8,128)(2,1)} fusion(bf16[32,2048,1408]{2,1,0:T(8,128)(2,1)} %param.18, f32[32,2,8,1408]{3,2,1,0:T(8,128)} %fusion.4, bf16[32,2,8,2048]{3,2,0,1:T(8,128)(2,1)S(1)} %all-to-all-done), kind=kOutput, calls=%fused_computation.10 | convolution fusion | flops 2957115392 | bytes 190971904 | tf_op jit(solution)/shard_map/lscd,ldf->lscf/dot_general | solution.py:42
  231.6 58.6 %fusion.12 = bf16[32,2,8,2048]{3,2,1,0:T(8,128)(2,1)S(1)} fusion(bf16[32,2,8,1408]{3,2,1,0:T(8,128)(2,1)} %fusion.9, bf16[32,1408,2048]{2,1,0:T(8,128)(2,1)} %param.19), kind=kOutput, calls=%fused_computation.11 | convolution fusion | flops 2953838592 | bytes 188088320 | tf_op jit(solution)/shard_map/lscf,lfd->lscd/dot_general | solution.py:44
  290.2 1.5 copy.24
  291.6 0.0 copy-start.8
  291.6 4.9 all-to-all-start.1
  296.6 0.0 copy-done.8
  296.6 0.1 copy.18
  296.7 0.0 copy-done.6
  296.7 0.1 copy.26
  296.8 0.1 reshape.68
  296.9 0.0 copy-done.7
  296.9 0.1 copy.17
  297.0 2.2 all-to-all-done.1
  299.2 1.7 copy.25
  300.9 1.1 gather_fusion.1
  302.1 0.0 copy-start.2
  302.1 0.3 reshape.67
  302.3 1.7 multiply_reduce_fusion
  304.1 198.2 %reduce-scatter.2.cloned.1.call-done = f32[32,2048]{1,0:T(8,128)} async-done(((f32[2048,2048]{1,0:T(8,128)}), f32[32,2048]{1,0:T(8,128)}) %reduce-scatter.2.cloned.1.call-update) | async-done | bytes 262160 | tf_op jit(solution)/shard_map/reduce_scatter | solution.py:32
  502.3 0.0 copy-done.2
  502.3 1.6 add_convert_fusion
  (11 shorter events, 0.0 us)
Async XLA Ops:
  6.5 90.3 %copy-start = (bf16[44,2048]{1,0:T(8,128)(2,1)S(1)}, bf16[44,2048]{1,0:T(8,128)(2,1)}, u32[]{:S(2)}) copy-start(bf16[44,2048]{1,0:T(8,128)(2,1)} %param.16) | copy-start | bytes 540676
  6.5 3.7 copy-start.1
  6.5 84.3 %all-gather.2.cloned.1.call-start = ((), (), s32[]{:S(2)}) async-start(), calls=%async_computation.3 | async-start | bytes 8519680 | tf_op jit(solution)/shard_map/all_gather | solution.py:30
  8.5 1.7 copy-start.5
  14.3 76.5 %copy-start.4 = (bf16[2048,44]{0,1:T(8,128)(2,1)S(1)}, bf16[2048,44]{0,1:T(8,128)(2,1)}, u32[]{:S(2)}) copy-start(bf16[2048,44]{0,1:T(8,128)(2,1)} %param.14) | copy-start | bytes 540676
  14.3 96.8 %all-to-all-start = ((bf16[32,2,8,2048]{3,2,0,1:T(8,128)(2,1)}), bf16[32,2,8,2048]{3,2,0,1:T(8,128)(2,1)S(1)}, u32[]{:S(2)}, u32[]{:S(2)}) async-start(bf16[32,2,8,2048]{3,2,0,1:T(8,128)(2,1)} %copy_select_fusion), calls=%async_computation.1 | async-start | bytes 4194304 | tf_op jit(solution)/shard_map/all_to_all | solution.py:40
  18.2 78.7 %copy-start.3 = (bf16[2048,44]{0,1:T(8,128)(2,1)S(1)}, bf16[2048,44]{0,1:T(8,128)(2,1)}, u32[]{:S(2)}) copy-start(bf16[2048,44]{0,1:T(8,128)(2,1)} %param.15) | copy-start | bytes 540676
  18.2 484.1 %reduce-scatter.2.cloned.1.call-start = ((), (), s32[]{:S(2)}) async-start(), calls=%async_computation.4 | async-start | bytes 17039360 | tf_op jit(solution)/shard_map/reduce_scatter | solution.py:32
  291.6 5.0 copy-start.8
  291.6 5.1 copy-start.6
  291.6 5.3 %copy-start.7 = (f32[32,6]{0,1:T(8,128)S(1)}, f32[32,6]{0,1:T(8,128)}, u32[]{:S(2)}) copy-start(f32[32,6]{0,1:T(8,128)} %param.12) | copy-start | bytes 2308
  291.6 7.5 %all-to-all-start.1 = ((bf16[32,2,8,2048]{3,2,0,1:T(8,128)(2,1)}), bf16[32,2,8,2048]{3,2,0,1:T(8,128)(2,1)}, u32[]{:S(2)}, u32[]{:S(2)}) async-start(bf16[32,2,8,2048]{3,2,0,1:T(8,128)(2,1)} %copy.24), calls=%async_computation.2 | async-start | bytes 4194304 | tf_op jit(solution)/shard_map/all_to_all | solution.py:45
  302.1 200.2 %copy-start.2 = (bf16[32,2048]{1,0:T(8,128)(2,1)S(1)}, bf16[32,2048]{1,0:T(8,128)(2,1)}, u32[]{:S(2)}) copy-start(bf16[32,2048]{1,0:T(8,128)(2,1)} %param.10) | copy-start | bytes 393220
Sparse Core Ops, SparseCore 0:
  10.2 80.5 all-gather.1
  111.2 390.9 reduce-scatter.1
where the time goes:
time: 511 us
  waiting for transfers between devices  273 us (53%)
  matrix products  199 us (39%)
  between operations  13.6 us (3%)
  local copies, waits for them, and re-layouts  9.08 us (2%)
  starting transfers between devices  9.06 us (2%)
  other arithmetic  6.22 us (1%)
    reduce_scatter x1, waiting for transfers between devices, local_layer(): lax.psum_scatter(part_sum, 'tp', scatter_dimension=0, tiled=True)  198 us
    all_gather x1, waiting for transfers between devices, local_layer(): group_rows = lax.all_gather(tokens, 'tp', axis=0, tiled=True)  72.4 us
    dot_general x1, matrix products, local_layer(): jnp.einsum('lscd,ldf->lscf', recv_rows, expert_w3, preferred_element_type...  60.7 us
    dot_general x1, matrix products, local_layer(): jnp.einsum('lscd,ldf->lscf', recv_rows, expert_w1, preferred_element_type...  59.7 us
    dot_general x1, matrix products, local_layer(): jnp.einsum('lscf,lfd->lscd', hidden, expert_w2, preferred_element_type=jn...  58.6 us
    dot_general x1, matrix products, swiglu_rows(): return jnp.dot(hidden, w_down, preferred_element_type=jnp.float32)  14.2 us
  transfers between devices with their start and end apart: 4, of which 3 were waited for; matrix products, arithmetic and copies ran while one was open for 42% of the time, Pallas kernels for 0%

commit v1 on v0

v1 whole, which is shorter than its diff:
```python
import functools

import jax
import jax.numpy as jnp
from jax import lax
from jax.experimental import pallas as pl
from jax.experimental.pallas import tpu as pltpu
from jax.sharding import PartitionSpec as P

MESH_ID = pl.DeviceIdType.MESH
BF16 = jnp.bfloat16
F32 = jnp.float32

CAP = 8
CUBE = 8
N_CHUNK = 4


def block_bounds(width, step):
    return [(lo, min(lo + step, width)) for lo in range(0, width, step)]


def silu(x):
    return x * jax.nn.sigmoid(x)


def moe_kernel(
    dims,
    tok_hbm, ids_hbm, slots_hbm, gates_hbm, sw1_hbm, sw3_hbm, sw2_hbm, ew1_hbm, ew3_hbm, ew2_hbm,
    out_ref,
    a_buf, b_buf, x_buf, xg_buf, h_buf, r_buf, w_buf, hs_buf, zs_buf, zr_buf, y_buf, rv_buf, p_buf, g_buf, gt_buf, m_buf, sw_buf, ids_buf, slots_buf, gates_buf,
    a_sem, b_sem, loc_sem, x_send, x_recv, fx_send, m_send, m_recv, fm_send, w_send, w_recv, z_send, z_recv, r_send, r_recv,
):
    tok_dev, d_model, ff, hid, top_k, n_loc = dims
    hid_pad = w_buf.shape[1] // CUBE
    half_rows = CUBE * tok_dev
    chunk_w = d_model // N_CHUNK
    n_exp = xg_buf.shape[0]
    src_rows = CUBE * CAP

    dp = lax.axis_index("dp")
    t = lax.axis_index("tp")
    core = lax.axis_index("ep")
    x, y, z = t % 4, (t // 4) % 4, t // 16
    parity = (x % 2) + 2 * (y % 2) + 4 * (z % 2)
    first_exp = parity * n_exp
    turn = 1 - 2 * core

    def flip(c, s):
        return (c + s * (1 - 2 * (c % 2)) + 4) % 4

    def chip(rel, s):
        cx = flip(x, s) if rel & 1 else x
        cy = flip(y, s) if rel & 2 else y
        cz = flip(z, s) if rel & 4 else z
        return cx + 4 * cy + 16 * cz

    def token_peer(rel):
        return (dp, chip(rel, turn), core)

    def weight_peer(rel):
        return (dp, chip(rel, -turn), core)

    other_core = (dp, t, 1 - core)

    def a_copies(i, slot):
        return (
            pltpu.make_async_copy(ew1_hbm.at[first_exp + i], a_buf.at[slot], a_sem.at[slot]),
            pltpu.make_async_copy(ew3_hbm.at[first_exp + i], a_buf.at[slot + 1], a_sem.at[slot + 1]),
        )

    def b_copy(n):
        slot = n % b_buf.shape[0]
        return pltpu.make_async_copy(ew2_hbm.at[pl.ds(first_exp, n_exp), :, pl.ds(n * chunk_w, chunk_w)], b_buf.at[slot], b_sem.at[slot])

    def rows(r):
        return pl.ds(r * tok_dev, tok_dev)

    tok_copy = pltpu.make_async_copy(tok_hbm, x_buf.at[0, rows(0)], loc_sem.at[0])
    tok_copy.start()
    meta_copies = [
        pltpu.make_async_copy(src, dst, loc_sem.at[1 + k])
        for k, (src, dst) in enumerate(((ids_hbm, ids_buf), (slots_hbm, slots_buf), (gates_hbm, gates_buf)))
    ]
    for c in meta_copies:
        c.start()
    w_copies = [
        pltpu.make_async_copy(src, sw_buf.at[third], loc_sem.at[4 + third])
        for third, src in enumerate((sw1_hbm, sw3_hbm, sw2_hbm))
    ]
    for c in w_copies:
        c.start()
    for i in range(2):
        for c in a_copies(i, 2 * i):
            c.start()
    b_copy(0).start()
    b_copy(1).start()

    barrier = pltpu.get_barrier_semaphore()
    peers = [token_peer(r) for r in range(1, CUBE)] + [weight_peer(1 << d) for d in range(3)] + [other_core]
    for peer in peers:
        pl.semaphore_signal(barrier, inc=1, device_id=peer, device_id_type=MESH_ID)

    m_buf[0, 0] = jnp.zeros(m_buf.shape[2:], F32)
    for c in meta_copies:
        c.wait()
    ids, slots = ids_buf[...], slots_buf[...]
    m_buf[0, 0, 0:top_k, 0:tok_dev] = jnp.where(slots >= 0, ids * CAP + slots, -1).astype(F32)
    m_buf[0, 0, 8 : 8 + top_k, 0:tok_dev] = gates_buf[...]
    tok_copy.wait()
    for third in range(3):
        w_copies[third].wait()
        w_buf[third, hid_pad - 16 : hid_pad, :] = jnp.zeros((16, d_model), BF16)
        w_buf[third, 0:hid, :] = sw_buf[third]
    pl.semaphore_wait(barrier, len(peers))

    def remote(src, dst, send, recv, peer):
        return pltpu.make_async_remote_copy(src_ref=src, dst_ref=dst, send_sem=send, recv_sem=recv, device_id=peer, device_id_type=MESH_ID)

    x_out = [remote(x_buf.at[0, rows(0)], x_buf.at[0, rows(r)], x_send.at[r], x_recv.at[0, r], token_peer(r)) for r in range(1, CUBE)]
    m_out = [remote(m_buf.at[0, 0], m_buf.at[0, r], m_send.at[r], m_recv.at[0, r], token_peer(r)) for r in range(1, CUBE)]
    x_fwd = [remote(x_buf.at[0, rows(r)], x_buf.at[1, rows(r)], fx_send.at[r], x_recv.at[1, r], other_core) for r in range(CUBE)]
    m_fwd = [remote(m_buf.at[0, r], m_buf.at[1, r], fm_send.at[r], m_recv.at[1, r], other_core) for r in range(CUBE)]

    def w_out(third, phase):
        dim_order = [(third + s) % 3 for s in range(3)]
        held = [0]
        for s in range(phase):
            held = held + [h | (1 << dim_order[s]) for h in held]
        bit = 1 << dim_order[phase]
        return [
            remote(
                w_buf.at[third, pl.ds(h * hid_pad, hid_pad)],
                w_buf.at[third, pl.ds((h | bit) * hid_pad, hid_pad)],
                w_send.at[third, h | bit],
                w_recv.at[third, h | bit],
                weight_peer(bit),
            )
            for h in held
        ]

    w_phases = [[c for third in range(3) for c in w_out(third, phase)] for phase in range(3)]

    for c in m_out + x_out:
        c.start()
    m_fwd[0].start()
    x_fwd[0].start()
    for c in w_phases[0]:
        c.start()
    for r in range(1, CUBE):
        m_out[r - 1].wait_recv()
        m_fwd[r].start()
        x_out[r - 1].wait_recv()
        x_fwd[r].start()
    for c in w_phases[0]:
        c.wait_recv()
    for c in w_phases[1]:
        c.start()
    for r in range(CUBE):
        m_fwd[r].wait_recv()
        x_fwd[r].wait_recv()

    lane = lax.broadcasted_iota(jnp.int32, (src_rows, half_rows), 1)
    row = lax.broadcasted_iota(jnp.int32, (src_rows, half_rows), 0)
    same_src = (row // CAP) == (lane // tok_dev)
    slot_of_row = row % CAP
    per_tile = 128 // tok_dev
    for half in range(2):
        code_tiles, gate_tiles = [], []
        for g in range(CUBE // per_tile):
            code_g = m_buf[half, g * per_tile, 0:8]
            gate_g = m_buf[half, g * per_tile, 8:16]
            for k in range(1, per_tile):
                code_g = code_g + pltpu.roll(m_buf[half, g * per_tile + k, 0:8], k * tok_dev, 1)
                gate_g = gate_g + pltpu.roll(m_buf[half, g * per_tile + k, 8:16], k * tok_dev, 1)
            code_tiles.append(code_g)
            gate_tiles.append(gate_g)
        codes = jnp.concatenate(code_tiles, axis=1)
        gate_rows = jnp.concatenate(gate_tiles, axis=1)
        for i in range(n_exp):
            want = ((core * n_loc + first_exp + i) * CAP + slot_of_row).astype(F32)
            want = jnp.where(same_src, want, -2.0)
            hit = jnp.zeros((src_rows, half_rows), F32)
            gate = jnp.zeros((src_rows, half_rows), F32)
            for j in range(top_k):
                match = want == codes[j : j + 1, :]
                hit = jnp.where(match, 1.0, hit)
                gate = jnp.where(match, gate_rows[j : j + 1, :], gate)
            p_buf[half, i * src_rows : (i + 1) * src_rows, :] = hit.astype(BF16)
            g_buf[i * src_rows : (i + 1) * src_rows, :] = gate
        rest = g_buf[...].T
        for k in range(3):
            part = rest.astype(BF16)
            gt_buf[half, k] = part
            rest = rest - part.astype(F32)
        for lo, hi in block_bounds(d_model, 512):
            picked = jnp.dot(p_buf[half], x_buf[half, :, lo:hi], preferred_element_type=F32).astype(BF16)
            for i in range(n_exp):
                xg_buf[i, half * src_rows : (half + 1) * src_rows, lo:hi] = picked[i * src_rows : (i + 1) * src_rows]
    b_copy(2).start()

    def expert_step(i, carry):
        slot = 2 * (i % 2)
        for c in a_copies(i, slot):
            c.wait()
        for lo, hi in block_bounds(ff, 512):
            gate_pre = jnp.dot(xg_buf[i], a_buf[slot, :, lo:hi], preferred_element_type=F32)
            up_pre = jnp.dot(xg_buf[i], a_buf[slot + 1, :, lo:hi], preferred_element_type=F32)
            h_buf[i, :, lo:hi] = (silu(gate_pre) * up_pre).astype(BF16)

        @pl.when(i < n_exp - 2)
        def _():
            for c in a_copies(i + 2, slot):
                c.start()

        @pl.when(i == 0)
        def _():
            for c in w_phases[1]:
                c.wait_recv()
            for c in w_phases[2]:
                c.start()

        return carry

    lax.fori_loop(0, n_exp, expert_step, 0)

    for c in w_phases[2]:
        c.wait_recv()
    nt = (((1,), (1,)), ((), ()))
    for lo, hi in block_bounds(CUBE * hid_pad, 128):
        gate_pre = lax.dot_general(x_buf[0], w_buf[0, lo:hi, :], nt, preferred_element_type=F32)
        up_pre = lax.dot_general(x_buf[0], w_buf[1, lo:hi, :], nt, preferred_element_type=F32)
        hs_buf[:, lo:hi] = (silu(gate_pre) * up_pre).astype(BF16)

    z_out = [remote(zs_buf.at[n], zr_buf.at[n], z_send.at[n], z_recv.at[n], other_core) for n in range(N_CHUNK)]
    r_out = [
        [remote(y_buf.at[n, rows(r)], rv_buf.at[n, rows(r)], r_send.at[n, r], r_recv.at[n, r], token_peer(r)) for r in range(1, CUBE)]
        for n in range(N_CHUNK)
    ]

    def finish_chunk(n):
        z_out[n].wait_recv()
        y_buf[n] = y_buf[n] + zr_buf[n]
        for c in r_out[n]:
            c.start()

    def combine(half):
        total = jnp.dot(gt_buf[half, 2], r_buf[half], preferred_element_type=F32)
        total = total + jnp.dot(gt_buf[half, 1], r_buf[half], preferred_element_type=F32)
        return total + jnp.dot(gt_buf[half, 0], r_buf[half], preferred_element_type=F32)

    for n in range(N_CHUNK):
        b_copy(n).wait()
        slot = n % b_buf.shape[0]

        def down_step(i, carry):
            res = jnp.dot(h_buf[i], b_buf[slot, i], preferred_element_type=F32).astype(BF16)
            r_buf[0, pl.ds(pl.multiple_of(i * src_rows, src_rows), src_rows), :] = res[:src_rows]
            r_buf[1, pl.ds(pl.multiple_of(i * src_rows, src_rows), src_rows), :] = res[src_rows:]
            return carry

        lax.fori_loop(0, n_exp, down_step, 0)
        if n + b_buf.shape[0] < N_CHUNK:
            b_copy(n + b_buf.shape[0]).start()
        zs_buf[n] = combine(1)
        z_out[n].start()
        shared = jnp.dot(hs_buf[...], w_buf[2, :, n * chunk_w : (n + 1) * chunk_w], preferred_element_type=F32)
        y_buf[n] = shared + combine(0)
        if n > 0:
            finish_chunk(n - 1)
    finish_chunk(N_CHUNK - 1)

    for n in range(N_CHUNK):
        cols = slice(n * chunk_w, (n + 1) * chunk_w)
        total = x_buf[0, 0:tok_dev, cols].astype(F32) + y_buf[n, 0:tok_dev]
        for r in range(1, CUBE):
            r_out[n][r - 1].wait_recv()
            total = total + rv_buf[n, r * tok_dev : (r + 1) * tok_dev]
        out_ref[:, cols] = total.astype(BF16)

    for c in m_out + x_out + m_fwd + x_fwd + [c for ph in w_phases for c in ph] + z_out + [c for ch in r_out for c in ch]:
        c.wait_send()


def solution(mesh):
    ep_size = mesh.shape["ep"]
    row_spec = P(("dp", "ep", "tp"), None)
    expert_spec = P("ep", None, None)

    def local_layer(tokens, expert_ids, gates, slots, shared_w1, shared_w3, shared_w2, expert_w1, expert_w3, expert_w2):
        tok_dev, d_model = tokens.shape
        top_k = expert_ids.shape[1]
        n_loc, _, ff = expert_w1.shape
        hid = shared_w2.shape[0]
        hid_pad = -(-hid // 16) * 16
        n_exp = n_loc // CUBE
        chunk_w = d_model // N_CHUNK
        half_rows = CUBE * tok_dev
        src_rows = CUBE * CAP
        dims = (tok_dev, d_model, ff, hid, top_k, n_loc)
        dma = pltpu.SemaphoreType.DMA
        scratch = [
            pltpu.VMEM((4, d_model, ff), BF16),
            pltpu.VMEM((3, n_exp, ff, chunk_w), BF16),
            pltpu.VMEM((2, half_rows, d_model), BF16),
            pltpu.VMEM((n_exp, 2 * src_rows, d_model), BF16),
            pltpu.VMEM((n_exp, 2 * src_rows, ff), BF16),
            pltpu.VMEM((2, n_exp * src_rows, chunk_w), BF16),
            pltpu.VMEM((3, CUBE * hid_pad, d_model), BF16),
            pltpu.VMEM((half_rows, CUBE * hid_pad), BF16),
            pltpu.VMEM((N_CHUNK, half_rows, chunk_w), F32),
            pltpu.VMEM((N_CHUNK, half_rows, chunk_w), F32),
            pltpu.VMEM((N_CHUNK, half_rows, chunk_w), F32),
            pltpu.VMEM((N_CHUNK, half_rows, chunk_w), F32),
            pltpu.VMEM((2, n_exp * src_rows, half_rows), BF16),
            pltpu.VMEM((n_exp * src_rows, half_rows), F32),
            pltpu.VMEM((2, 3, half_rows, n_exp * src_rows), BF16),
            pltpu.VMEM((2, CUBE, 16, 128), F32),
            pltpu.VMEM((3, hid, d_model), BF16),
            pltpu.VMEM((top_k, tok_dev), jnp.int32),
            pltpu.VMEM((top_k, tok_dev), jnp.int32),
            pltpu.VMEM((top_k, tok_dev), F32),
            dma((4,)), dma((3,)), dma((7,)),
            dma((CUBE,)), dma((2, CUBE)), dma((CUBE,)),
            dma((CUBE,)), dma((2, CUBE)), dma((CUBE,)),
            dma((3, CUBE)), dma((3, CUBE)),
            dma((N_CHUNK,)), dma((N_CHUNK,)),
            dma((N_CHUNK, CUBE)), dma((N_CHUNK, CUBE)),
        ]
        any_spec = pl.BlockSpec(memory_space=pl.ANY)
        return pl.pallas_call(
            functools.partial(moe_kernel, dims),
            out_shape=jax.ShapeDtypeStruct((tok_dev, d_model), BF16),
            in_specs=[any_spec] * 10,
            out_specs=pl.BlockSpec(memory_space=pltpu.VMEM),
            scratch_shapes=scratch,
            compiler_params=pltpu.CompilerParams(collective_id=0, has_side_effects=True, vmem_limit_bytes=67043328),
        )(tokens, expert_ids.T, slots.T, gates.T, shared_w1.T, shared_w3.T, shared_w2, expert_w1, expert_w3, expert_w2)

    return jax.shard_map(local_layer, mesh=mesh, in_specs=(row_spec, row_spec, row_spec, row_spec, P(None, "tp"), P(None, "tp"), P("tp", None), expert_spec, expert_spec, expert_spec), out_specs=row_spec, check_vma=False)
```

time: 511 us -> 72.8 us (0.14)
  the two profiles are of different devices: /device:TPU:0 before, /device:TPU:1 now
where the time goes in v1:
time: 72.8 us; the launch traced here: 72.1 us
  Pallas kernels  70.6 us (97%)
  local copies, waits for them, and re-layouts  1.57 us (2%)
    pallas_call x1, Pallas kernels, local_layer(): pl.pallas_call(functools.partial(moe_kernel, dims), out_shape=jax.ShapeDt...  70.6 us
    unnamed x1, local copies, waits for them, and re-layouts  1.57 us

profile of v1, /device:TPU:1, one launch (start us, length us, event | category | flops | bytes accessed | tf_op | source)
XLA Modules:
  0.0 72.1 jit_solution(5324970306807708000)
XLA Ops:
  0.0 70.6 %shard_map.100 = bf16[32,2048]{1,0:T(8,128)(2,1)} custom-call(bf16[32,2048]{1,0:T(8,128)(2,1)} %tok_hbm.1, s32[6,32]{1,0:T(8,128)} %bitcast.7, s32[6,32]{1,0:T(8,128)} %bitcast.8, f32[6,32]{1,0:T(8,128)} %bitcast.9, bf16[44,2048]{1,0:T(8,128)(2,1)} %bitcast.5, bf16[44,2048]{1,0:T(8,128)(2,1)} %bitcast.6, bf16[44,2048]{1,0:T(8,128)(2,1)} %sw2_hbm.1, ...), custom_call_target="tpu_custom_call" | custom-call | tf_op jit(solution)/shard_map/pallas_call | solution.py:331
  70.6 1.6 %copy.12 = bf16[32,2048]{1,0:T(8,128)(2,1)} copy(bf16[32,2048]{1,0:T(8,128)(2,1)} %shard_map.100) | data formatting | bytes 262144

commit v2 on v1

--- a/solution.py
+++ b/solution.py
@@ -90,14 +90,14 @@
     ]
     for c in w_copies:
         c.start()
-    for i in range(2):
-        for c in a_copies(i, 2 * i):
-            c.start()
-    b_copy(0).start()
-    b_copy(1).start()
+
+    def start_expert(i, slot):
+        for c in a_copies(i, slot):
+            c.start()
+
 
     barrier = pltpu.get_barrier_semaphore()
-    peers = [token_peer(r) for r in range(1, CUBE)] + [weight_peer(1 << d) for d in range(3)] + [other_core]
+    peers = [token_peer(r) for r in (1, 2, 4, 7)] + [weight_peer(1 << d) for d in range(3)] + [other_core]
     for peer in peers:
         pl.semaphore_signal(barrier, inc=1, device_id=peer, device_id_type=MESH_ID)
 
@@ -112,53 +112,83 @@
         w_copies[third].wait()
         w_buf[third, hid_pad - 16 : hid_pad, :] = jnp.zeros((16, d_model), BF16)
         w_buf[third, 0:hid, :] = sw_buf[third]
+    start_expert(0, 0)
+    start_expert(1, 2)
+    b_copy(0).start()
+    b_copy(1).start()
     pl.semaphore_wait(barrier, len(peers))
 
     def remote(src, dst, send, recv, peer):
         return pltpu.make_async_remote_copy(src_ref=src, dst_ref=dst, send_sem=send, recv_sem=recv, device_id=peer, device_id_type=MESH_ID)
 
-    x_out = [remote(x_buf.at[0, rows(0)], x_buf.at[0, rows(r)], x_send.at[r], x_recv.at[0, r], token_peer(r)) for r in range(1, CUBE)]
-    m_out = [remote(m_buf.at[0, 0], m_buf.at[0, r], m_send.at[r], m_recv.at[0, r], token_peer(r)) for r in range(1, CUBE)]
-    x_fwd = [remote(x_buf.at[0, rows(r)], x_buf.at[1, rows(r)], fx_send.at[r], x_recv.at[1, r], other_core) for r in range(CUBE)]
-    m_fwd = [remote(m_buf.at[0, r], m_buf.at[1, r], fm_send.at[r], m_recv.at[1, r], other_core) for r in range(CUBE)]
-
-    def w_out(third, phase):
-        dim_order = [(third + s) % 3 for s in range(3)]
-        held = [0]
-        for s in range(phase):
-            held = held + [h | (1 << dim_order[s]) for h in held]
-        bit = 1 << dim_order[phase]
-        return [
-            remote(
-                w_buf.at[third, pl.ds(h * hid_pad, hid_pad)],
-                w_buf.at[third, pl.ds((h | bit) * hid_pad, hid_pad)],
-                w_send.at[third, h | bit],
-                w_recv.at[third, h | bit],
-                weight_peer(bit),
-            )
-            for h in held
-        ]
-
-    w_phases = [[c for third in range(3) for c in w_out(third, phase)] for phase in range(3)]
-
-    for c in m_out + x_out:
+    def x_copies(src, dst, peer):
+        return (
+            remote(m_buf.at[0, src], m_buf.at[0, dst], m_send.at[dst], m_recv.at[0, dst], peer),
+            remote(x_buf.at[0, rows(src)], x_buf.at[0, rows(dst)], x_send.at[dst], x_recv.at[0, dst], peer),
+        )
+
+    def next_bit(bit):
+        return 1 if bit == 4 else 2 * bit
+
+    x_in = {bit: x_copies(0, bit, token_peer(bit)) for bit in (1, 2, 4)}
+    x_hop = {bit: x_copies(bit, bit | next_bit(bit), token_peer(next_bit(bit))) for bit in (1, 2, 4)}
+    x_far = x_copies(0, 7, token_peer(7))
+    x_fwd = [
+        (
+            remote(m_buf.at[0, r], m_buf.at[1, r], fm_send.at[r], m_recv.at[1, r], other_core),
+            remote(x_buf.at[0, rows(r)], x_buf.at[1, rows(r)], fx_send.at[r], x_recv.at[1, r], other_core),
+        )
+        for r in range(CUBE)
+    ]
+
+    def w_copy(third, src, bit):
+        dst = src | bit
+        return remote(
+            w_buf.at[third, pl.ds(src * hid_pad, hid_pad)],
+            w_buf.at[third, pl.ds(dst * hid_pad, hid_pad)],
+            w_send.at[third, dst],
+            w_recv.at[third, dst],
+            weight_peer(bit),
+        )
+
+    orders = [[1 << ((third + k) % 3) for k in range(3)] for third in range(3)]
+    w_own = [[w_copy(third, 0, orders[third][k]) for third in range(3)] for k in range(3)]
+    w_mid = [
+        [w_copy(third, orders[third][0], orders[third][1]) for third in range(3)],
+        [w_copy(third, orders[third][0], orders[third][2]) for third in range(3)],
+        [w_copy(third, orders[third][1], orders[third][2]) for third in range(3)],
+    ]
+    w_last = [w_copy(third, orders[third][0] | orders[third][1], orders[third][2]) for third in range(3)]
+
+    for bit in (1, 2, 4):
+        for c in x_in[bit]:
+            c.start()
+    for c in x_far + x_fwd[0]:
         c.start()
-    m_fwd[0].start()
-    x_fwd[0].start()
-    for c in w_phases[0]:
+    for group in w_own:
+        for c in group:
+            c.start()
+    for bit in (1, 2, 4):
+        for c in x_in[bit]:
+            c.wait_recv()
+        for c in x_hop[bit]:
+            c.start()
+        for c in x_fwd[bit]:
+            c.start()
+    for bit in (1, 2, 4):
+        r = bit | next_bit(bit)
+        for c in x_hop[bit]:
+            c.wait_recv()
+        for c in x_fwd[r]:
+            c.start()
+    for c in x_far:
+        c.wait_recv()
+    for c in x_fwd[7]:
         c.start()
-    for r in range(1, CUBE):
-        m_out[r - 1].wait_recv()
-        m_fwd[r].start()
-        x_out[r - 1].wait_recv()
-        x_fwd[r].start()
-    for c in w_phases[0]:
-        c.wait_recv()
-    for c in w_phases[1]:
-        c.start()
-    for r in range(CUBE):
-        m_fwd[r].wait_recv()
-        x_fwd[r].wait_recv()
+    b_copy(2).start()
+    for pair in x_fwd:
+        for c in pair:
+            c.wait_recv()
 
     lane = lax.broadcasted_iota(jnp.int32, (src_rows, half_rows), 1)
     row = lax.broadcasted_iota(jnp.int32, (src_rows, half_rows), 0)
@@ -197,7 +227,12 @@
             picked = jnp.dot(p_buf[half], x_buf[half, :, lo:hi], preferred_element_type=F32).astype(BF16)
             for i in range(n_exp):
                 xg_buf[i, half * src_rows : (half + 1) * src_rows, lo:hi] = picked[i * src_rows : (i + 1) * src_rows]
-    b_copy(2).start()
+    for k in range(2):
+        for c in w_own[k]:
+            c.wait_recv()
+    for group in w_mid:
+        for c in group:
+            c.start()
 
     def expert_step(i, carry):
         slot = 2 * (i % 2)
@@ -210,21 +245,20 @@
 
         @pl.when(i < n_exp - 2)
         def _():
-            for c in a_copies(i + 2, slot):
-                c.start()
+            start_expert(i + 2, slot)
 
         @pl.when(i == 0)
         def _():
-            for c in w_phases[1]:
+            for c in w_mid[0]:
                 c.wait_recv()
-            for c in w_phases[2]:
+            for c in w_last:
                 c.start()
 
         return carry
 
     lax.fori_loop(0, n_exp, expert_step, 0)
 
-    for c in w_phases[2]:
+    for c in w_own[2] + w_mid[1] + w_mid[2] + w_last:
         c.wait_recv()
     nt = (((1,), (1,)), ((), ()))
     for lo, hi in block_bounds(CUBE * hid_pad, 128):
@@ -233,16 +267,26 @@
         hs_buf[:, lo:hi] = (silu(gate_pre) * up_pre).astype(BF16)
 
     z_out = [remote(zs_buf.at[n], zr_buf.at[n], z_send.at[n], z_recv.at[n], other_core) for n in range(N_CHUNK)]
-    r_out = [
-        [remote(y_buf.at[n, rows(r)], rv_buf.at[n, rows(r)], r_send.at[n, r], r_recv.at[n, r], token_peer(r)) for r in range(1, CUBE)]
-        for n in range(N_CHUNK)
-    ]
-
-    def finish_chunk(n):
+
+    def r_copy(n, r, peer):
+        return remote(y_buf.at[n, rows(r)], rv_buf.at[n, rows(r)], r_send.at[n, r], r_recv.at[n, r], peer)
+
+    r_via = [{bit: r_copy(n, bit | next_bit(bit), token_peer(bit)) for bit in (1, 2, 4)} for n in range(N_CHUNK)]
+    r_home = [{r: r_copy(n, r, token_peer(r)) for r in (1, 2, 4, 7)} for n in range(N_CHUNK)]
+
+    def chunk_to_cube(n):
         z_out[n].wait_recv()
         y_buf[n] = y_buf[n] + zr_buf[n]
-        for c in r_out[n]:
-            c.start()
+        for bit in (1, 2, 4):
+            r_via[n][bit].start()
+        r_home[n][7].start()
+
+    def chunk_to_home(n):
+        for bit in (1, 2, 4):
+            mine, via = next_bit(bit), bit | next_bit(bit)
+            r_via[n][bit].wait_recv()
+            y_buf[n, rows(mine), :] = y_buf[n, rows(mine), :] + rv_buf[n, rows(via), :]
+            r_home[n][mine].start()
 
     def combine(half):
         total = jnp.dot(gt_buf[half, 2], r_buf[half], preferred_element_type=F32)
@@ -253,13 +297,13 @@
         b_copy(n).wait()
         slot = n % b_buf.shape[0]
 
-        def down_step(i, carry):
+        def down_step(i):
             res = jnp.dot(h_buf[i], b_buf[slot, i], preferred_element_type=F32).astype(BF16)
-            r_buf[0, pl.ds(pl.multiple_of(i * src_rows, src_rows), src_rows), :] = res[:src_rows]
-            r_buf[1, pl.ds(pl.multiple_of(i * src_rows, src_rows), src_rows), :] = res[src_rows:]
-            return carry
-
-        lax.fori_loop(0, n_exp, down_step, 0)
+            r_buf[0, i * src_rows : (i + 1) * src_rows, :] = res[:src_rows]
+            r_buf[1, i * src_rows : (i + 1) * src_rows, :] = res[src_rows:]
+
+        for i in range(n_exp):
+            down_step(i)
         if n + b_buf.shape[0] < N_CHUNK:
             b_copy(n + b_buf.shape[0]).start()
         zs_buf[n] = combine(1)
@@ -267,19 +311,27 @@
         shared = jnp.dot(hs_buf[...], w_buf[2, :, n * chunk_w : (n + 1) * chunk_w], preferred_element_type=F32)
         y_buf[n] = shared + combine(0)
         if n > 0:
-            finish_chunk(n - 1)
-    finish_chunk(N_CHUNK - 1)
+            chunk_to_cube(n - 1)
+        if n > 1:
+            chunk_to_home(n - 2)
+    chunk_to_cube(N_CHUNK - 1)
+    chunk_to_home(N_CHUNK - 2)
+    chunk_to_home(N_CHUNK - 1)
 
     for n in range(N_CHUNK):
         cols = slice(n * chunk_w, (n + 1) * chunk_w)
         total = x_buf[0, 0:tok_dev, cols].astype(F32) + y_buf[n, 0:tok_dev]
-        for r in range(1, CUBE):
-            r_out[n][r - 1].wait_recv()
+        for r in (1, 2, 4, 7):
+            r_home[n][r].wait_recv()
             total = total + rv_buf[n, r * tok_dev : (r + 1) * tok_dev]
         out_ref[:, cols] = total.astype(BF16)
 
-    for c in m_out + x_out + m_fwd + x_fwd + [c for ph in w_phases for c in ph] + z_out + [c for ch in r_out for c in ch]:
-        c.wait_send()
+    pairs = list(x_in.values()) + list(x_hop.values()) + [x_far] + x_fwd
+    groups = w_own + w_mid + [w_last, z_out]
+    chunks = [list(ch.values()) for ch in r_via + r_home]
+    for group in pairs + groups + chunks:
+        for c in group:
+            c.wait_send()
 
 
 def solution(mesh):

time: 72.8 us -> 59.8 us (0.82)
  Pallas kernels: 70.6 us -> 58.1 us
    pallas_call x1, Pallas kernels: 70.6 us -> 58.1 us  [local_layer(): pl.pallas_call(functools.partial(moe_kernel, dims), out_shape=jax.ShapeDt...]
where the time goes in v2:
time: 59.8 us; the launch traced here: 59.6 us
  Pallas kernels  58.1 us (97%)
  local copies, waits for them, and re-layouts  1.57 us (3%)
    pallas_call x1, Pallas kernels, local_layer(): pl.pallas_call(functools.partial(moe_kernel, dims), out_shape=jax.ShapeDt...  58.1 us
    unnamed x1, local copies, waits for them, and re-layouts  1.57 us

profile of v2, /device:TPU:1, one launch (start us, length us, event | category | flops | bytes accessed | tf_op | source)
XLA Modules:
  0.0 59.6 jit_solution(11218337796002872231)
XLA Ops:
  0.0 58.1 %shard_map.100 = bf16[32,2048]{1,0:T(8,128)(2,1)} custom-call(bf16[32,2048]{1,0:T(8,128)(2,1)} %tok_hbm.1, s32[6,32]{1,0:T(8,128)} %bitcast.7, s32[6,32]{1,0:T(8,128)} %bitcast.8, f32[6,32]{1,0:T(8,128)} %bitcast.9, bf16[44,2048]{1,0:T(8,128)(2,1)} %bitcast.5, bf16[44,2048]{1,0:T(8,128)(2,1)} %bitcast.6, bf16[44,2048]{1,0:T(8,128)(2,1)} %sw2_hbm.1, ...), custom_call_target="tpu_custom_call" | custom-call | tf_op jit(solution)/shard_map/pallas_call | solution.py:383
  58.1 1.6 %copy.12 = bf16[32,2048]{1,0:T(8,128)(2,1)} copy(bf16[32,2048]{1,0:T(8,128)(2,1)} %shard_map.100) | data formatting | bytes 262144

commit v3 on v2

--- a/solution.py
+++ b/solution.py
@@ -63,11 +63,15 @@
 
     other_core = (dp, t, 1 - core)
 
-    def a_copies(i, slot):
-        return (
-            pltpu.make_async_copy(ew1_hbm.at[first_exp + i], a_buf.at[slot], a_sem.at[slot]),
-            pltpu.make_async_copy(ew3_hbm.at[first_exp + i], a_buf.at[slot + 1], a_sem.at[slot + 1]),
-        )
+    ff_blocks = block_bounds(ff, 512)
+
+    def a_copies(i, blk):
+        slot = 2 * (i % 2)
+        cols = pl.ds(ff_blocks[blk][0], ff_blocks[blk][1] - ff_blocks[blk][0])
+        return [
+            pltpu.make_async_copy(src.at[first_exp + i, :, cols], a_buf.at[slot + k, :, cols], a_sem.at[slot + k, blk])
+            for k, src in enumerate((ew1_hbm, ew3_hbm))
+        ]
 
     def b_copy(n):
         slot = n % b_buf.shape[0]
@@ -91,9 +95,10 @@
     for c in w_copies:
         c.start()
 
-    def start_expert(i, slot):
-        for c in a_copies(i, slot):
-            c.start()
+    def start_expert(i):
+        for blk in range(len(ff_blocks)):
+            for c in a_copies(i, blk):
+                c.start()
 
 
     barrier = pltpu.get_barrier_semaphore()
@@ -112,8 +117,8 @@
         w_copies[third].wait()
         w_buf[third, hid_pad - 16 : hid_pad, :] = jnp.zeros((16, d_model), BF16)
         w_buf[third, 0:hid, :] = sw_buf[third]
-    start_expert(0, 0)
-    start_expert(1, 2)
+    start_expert(0)
+    start_expert(1)
     b_copy(0).start()
     b_copy(1).start()
     pl.semaphore_wait(barrier, len(peers))
@@ -186,9 +191,11 @@
     for c in x_fwd[7]:
         c.start()
     b_copy(2).start()
-    for pair in x_fwd:
-        for c in pair:
-            c.wait_recv()
+    for c in w_own[0]:
+        c.wait_recv()
+    for group in w_mid[:2]:
+        for c in group:
+            c.start()
 
     lane = lax.broadcasted_iota(jnp.int32, (src_rows, half_rows), 1)
     row = lax.broadcasted_iota(jnp.int32, (src_rows, half_rows), 0)
@@ -196,6 +203,10 @@
     slot_of_row = row % CAP
     per_tile = 128 // tok_dev
     for half in range(2):
+        if half == 1:
+            for pair in x_fwd:
+                for c in pair:
+                    c.wait_recv()
         code_tiles, gate_tiles = [], []
         for g in range(CUBE // per_tile):
             code_g = m_buf[half, g * per_tile, 0:8]
@@ -227,41 +238,32 @@
             picked = jnp.dot(p_buf[half], x_buf[half, :, lo:hi], preferred_element_type=F32).astype(BF16)
             for i in range(n_exp):
                 xg_buf[i, half * src_rows : (half + 1) * src_rows, lo:hi] = picked[i * src_rows : (i + 1) * src_rows]
-    for k in range(2):
-        for c in w_own[k]:
-            c.wait_recv()
-    for group in w_mid:
-        for c in group:
-            c.start()
-
-    def expert_step(i, carry):
+    for c in w_own[1]:
+        c.wait_recv()
+    for c in w_mid[2]:
+        c.start()
+
+    for i in range(n_exp):
         slot = 2 * (i % 2)
-        for c in a_copies(i, slot):
-            c.wait()
-        for lo, hi in block_bounds(ff, 512):
+        for blk, (lo, hi) in enumerate(ff_blocks):
+            for c in a_copies(i, blk):
+                c.wait()
             gate_pre = jnp.dot(xg_buf[i], a_buf[slot, :, lo:hi], preferred_element_type=F32)
             up_pre = jnp.dot(xg_buf[i], a_buf[slot + 1, :, lo:hi], preferred_element_type=F32)
             h_buf[i, :, lo:hi] = (silu(gate_pre) * up_pre).astype(BF16)
-
-        @pl.when(i < n_exp - 2)
-        def _():
-            start_expert(i + 2, slot)
-
-        @pl.when(i == 0)
-        def _():
+            if i + 2 < n_exp:
+                for c in a_copies(i + 2, blk):
+                    c.start()
+        if i == 1:
             for c in w_mid[0]:
                 c.wait_recv()
             for c in w_last:
                 c.start()
 
-        return carry
-
-    lax.fori_loop(0, n_exp, expert_step, 0)
-
     for c in w_own[2] + w_mid[1] + w_mid[2] + w_last:
         c.wait_recv()
     nt = (((1,), (1,)), ((), ()))
-    for lo, hi in block_bounds(CUBE * hid_pad, 128):
+    for lo, hi in block_bounds(CUBE * hid_pad, 256):
         gate_pre = lax.dot_general(x_buf[0], w_buf[0, lo:hi, :], nt, preferred_element_type=F32)
         up_pre = lax.dot_general(x_buf[0], w_buf[1, lo:hi, :], nt, preferred_element_type=F32)
         hs_buf[:, lo:hi] = (silu(gate_pre) * up_pre).astype(BF16)
@@ -310,13 +312,13 @@
         z_out[n].start()
         shared = jnp.dot(hs_buf[...], w_buf[2, :, n * chunk_w : (n + 1) * chunk_w], preferred_element_type=F32)
         y_buf[n] = shared + combine(0)
-        if n > 0:
-            chunk_to_cube(n - 1)
         if n > 1:
-            chunk_to_home(n - 2)
+            chunk_to_cube(n - 2)
+    chunk_to_cube(N_CHUNK - 2)
+    chunk_to_home(0)
     chunk_to_cube(N_CHUNK - 1)
-    chunk_to_home(N_CHUNK - 2)
-    chunk_to_home(N_CHUNK - 1)
+    for n in range(1, N_CHUNK):
+        chunk_to_home(n)
 
     for n in range(N_CHUNK):
         cols = slice(n * chunk_w, (n + 1) * chunk_w)
@@ -372,7 +374,7 @@
             pltpu.VMEM((top_k, tok_dev), jnp.int32),
             pltpu.VMEM((top_k, tok_dev), jnp.int32),
             pltpu.VMEM((top_k, tok_dev), F32),
-            dma((4,)), dma((3,)), dma((7,)),
+            dma((4, len(block_bounds(ff, 512)))), dma((3,)), dma((7,)),
             dma((CUBE,)), dma((2, CUBE)), dma((CUBE,)),
             dma((CUBE,)), dma((2, CUBE)), dma((CUBE,)),
             dma((3, CUBE)), dma((3, CUBE)),

time: 59.8 us -> 54 us (0.903)
  Pallas kernels: 58.1 us -> 52.2 us
    pallas_call x1, Pallas kernels: 58.1 us -> 52.2 us  [local_layer(): pl.pallas_call(functools.partial(moe_kernel, dims), out_shape=jax.ShapeDt...]
where the time goes in v3:
time: 54 us; the launch traced here: 53.8 us
  Pallas kernels  52.2 us (97%)
  local copies, waits for them, and re-layouts  1.57 us (3%)
    pallas_call x1, Pallas kernels, local_layer(): pl.pallas_call(functools.partial(moe_kernel, dims), out_shape=jax.ShapeDt...  52.2 us
    unnamed x1, local copies, waits for them, and re-layouts  1.57 us

profile of v3, /device:TPU:1, one launch (start us, length us, event | category | flops | bytes accessed | tf_op | source)
XLA Modules:
  0.0 53.8 jit_solution(17252334922185791670)
XLA Ops:
  0.0 52.2 %shard_map.100 = bf16[32,2048]{1,0:T(8,128)(2,1)} custom-call(bf16[32,2048]{1,0:T(8,128)(2,1)} %tok_hbm.1, s32[6,32]{1,0:T(8,128)} %bitcast.7, s32[6,32]{1,0:T(8,128)} %bitcast.8, f32[6,32]{1,0:T(8,128)} %bitcast.9, bf16[44,2048]{1,0:T(8,128)(2,1)} %bitcast.5, bf16[44,2048]{1,0:T(8,128)(2,1)} %bitcast.6, bf16[44,2048]{1,0:T(8,128)(2,1)} %sw2_hbm.1, ...), custom_call_target="tpu_custom_call" | custom-call | tf_op jit(solution)/shard_map/pallas_call | solution.py:385
  52.3 1.6 %copy.12 = bf16[32,2048]{1,0:T(8,128)(2,1)} copy(bf16[32,2048]{1,0:T(8,128)(2,1)} %shard_map.100) | data formatting | bytes 262144
